TPU v7x, 32 devices: a whole 2x2x4 slice. The times are simulated.
32 devices in a mesh: dp: 4 (over x, core), vocab: 8 (over z, y).
Axes of the slice: x: 2, y: 2, z: 4, core: 2. Of those that a mesh axis runs over, the one named last changes fastest.
Arguments:
- hidden: bfloat16 [128, 8192], P(('dp', 'vocab')), may hold values from -350 to 350
- lm_head: bfloat16 [8192, 128256], P(None, ('dp', 'vocab')), may hold values from -0.0625 to 0.0625
- targets: int32 [128], P(('dp', 'vocab')), may hold values from 0 to 128255
- segment: int32 [128], P(('dp', 'vocab')), may hold values from 0 to 32, as said below
- pad_mask: int32 [128], P(('dp', 'vocab')), may hold values from 0 to 1, as said below
- seq_bench: int32 [33], replicated, may hold values from 0 to 7
Outputs:
- token_nll: float32 [128], P(('dp', 'vocab'))
- bench_total: float32 [8], replicated
- bench_count: float32 [8], replicated
Inputs may be any that keep to these rules, and one draw needn't show every extreme that they name: `segment`: sequence numbers never fall along the pack; each aligned block of 4 tokens holds exactly one place inside it where the number rises by one, and the number does not change between one block's last token and the next block's first. `pad_mask`: the last token of each aligned block of 4 tokens is real.
All inputs are finite; a program needn't handle non-finite values.
Results may differ from a plain program's by a relative error of at most 0.0003.
Values may be sent and summed in bfloat16 or wider, within the bound.
No kernel may reach another device: no remote copies, remote signals or barrier semaphores. Data moves between devices by JAX's collectives and lax.ppermute only.
A program may use at most 128 MiB of HBM per device.

v0:
```python
from functools import partial

import jax
import jax.numpy as jnp
from jax import lax
from jax.sharding import PartitionSpec as P

NBENCH = 8


def from_behind(value, axis, steps):
    count = lax.axis_size(axis)
    leading, last = (max(0, -steps), min(count, count - steps))
    return lax.ppermute(value, axis, [(source, source + steps) for source in range(leading, last)])


def shard_stats(piece, start, lm_head, all_targets, col_start):
    logits = jnp.dot(piece, lm_head, preferred_element_type=jnp.float32)
    row_top = jnp.max(logits, axis=1)
    expsum = jnp.sum(jnp.exp(logits - row_top[:, None]), axis=1)
    wanted = all_targets - col_start
    columns = lax.broadcasted_iota(jnp.int32, logits.shape, 1)
    picked = jnp.sum(jnp.where(columns == wanted[:, None], logits, 0.0), axis=1)
    return jnp.stack([row_top, expsum, picked], axis=0)


def global_top(stats):
    return lax.pmax(stats[0], ("dp", "vocab"))


def body(hidden, lm_head, targets, segment, pad_mask, seq_bench):
    tok_dev = hidden.shape[0]
    voc_dev = lm_head.shape[1]
    own_index = lax.axis_index(("dp", "vocab"))
    col_start = own_index * voc_dev
    row_start = own_index * tok_dev
    all_targets = lax.all_gather(targets, ("dp", "vocab"), axis=0, tiled=True)
    per_piece = partial(shard_stats, lm_head=lm_head, all_targets=all_targets, col_start=col_start)
    stats = per_piece(lax.all_gather(hidden, ("dp", "vocab"), axis=0, tiled=True), jnp.int32(0))
    top_all = global_top(stats)
    total_all, picked_all = lax.psum(
        (stats[1] * jnp.exp(stats[0] - top_all), stats[2]), ("dp", "vocab")
    )
    top = lax.dynamic_slice_in_dim(top_all, row_start, tok_dev, 0)
    total = lax.dynamic_slice_in_dim(total_all, row_start, tok_dev, 0)
    picked = lax.dynamic_slice_in_dim(picked_all, row_start, tok_dev, 0)
    token_nll = top + jnp.log(total) - picked
    next_first = from_behind(segment[:1] + 1, ("dp", "vocab"), -1)
    following = jnp.concatenate([segment[1:] + 1, next_first])
    keep = (pad_mask * (segment + 1 == following).astype(jnp.int32)).astype(jnp.float32)
    seq_count = seq_bench.shape[0]
    seq_hot = segment[:, None] == lax.broadcasted_iota(jnp.int32, (1, seq_count), 1)
    bench_of = jnp.sum(jnp.where(seq_hot, seq_bench[None, :], 0), axis=1)
    bench_hot = (bench_of[:, None] == lax.broadcasted_iota(jnp.int32, (1, NBENCH), 1)).astype(
        jnp.float32
    )
    weighted = keep * token_nll
    bench_total, bench_count = lax.psum(
        (
            jnp.sum(bench_hot * weighted[:, None], axis=0),
            jnp.sum(bench_hot * keep[:, None], axis=0),
        ),
        ("dp", "vocab"),
    )
    return (token_nll, bench_total, bench_count)


def solution(mesh):
    in_specs = (
        P(("dp", "vocab"), None),
        P(None, ("dp", "vocab")),
        P(("dp", "vocab")),
        P(("dp", "vocab")),
        P(("dp", "vocab")),
        P(),
    )
    out_specs = (P(("dp", "vocab")), P(), P())
    return jax.shard_map(body, mesh=mesh, in_specs=in_specs, out_specs=out_specs, check_vma=False)
```

profile of v0, /device:TPU:0, one launch (start us, length us, event | category | flops | bytes accessed | tf_op | source)
XLA Modules:
  0.0 228.6 jit_solution(5779471022666829221)
XLA Ops:
  7.2 0.0 all-gather.3.cloned.1.call-start
  7.2 0.7 all-gather.3.cloned.1.call-update
  8.5 1.3 collective-permute-start
  9.9 0.9 dynamic-update-slice
  10.7 44.3 %all-reduce = s32[128]{0:T(128)S(1)} all-reduce(s32[128]{0:T(128)S(1)} %dynamic-update-slice), channel_id=1, replica_groups=mesh['dp'=4,'vocab'=8] {'dp','vocab'}, use_global_device_ids=true, to_apply=%add | all-reduce | flops 128 | bytes 1024
  55.1 0.9 select_reduce_fusion.3
  55.9 0.7 slice_add_fusion
  56.6 13.5 %all-gather.3.cloned.1.call-done = bf16[32,4,8192]{2,1,0:T(4,128)(2,1)} async-done(((bf16[1,4,8192]{2,1,0:T(4,128)(2,1)}), bf16[32,4,8192]{2,1,0:T(4,128)(2,1)}) %all-gather.3.cloned.1.call-update) | async-done | bytes 2097168 | tf_op jit(solution)/shard_map/all_gather | solution.py:39
  70.1 2.5 %reshape.16 = bf16[128,8192]{1,0:T(8,128)(2,1)S(1)} reshape(bf16[32,4,8192]{2,1,0:T(4,128)(2,1)} %all-gather.3.cloned.1.call-done) | data formatting | bytes 4194304
  72.7 27.4 %fusion.3 = (f32[128]{0:T(128)S(1)}, f32[128,4008]{0,1:T(8,128)}) fusion(bf16[128,8192]{1,0:T(8,128)(2,1)S(1)} %reshape.16, bf16[8192,4008]{0,1:T(8,128)(2,1)} %param.7), kind=kOutput, calls=%fused_computation.15 | convolution fusion | flops 8405898240 | bytes 69816832 | tf_op jit(solution)/shard_map/dot_general | solution.py:18
  100.1 0.0 copy-start
  100.1 0.0 copy-start.1
  100.1 38.3 %pmax.7 = f32[128]{0:T(128)S(1)} all-reduce(f32[128]{0:T(128)S(1)} %get-tuple-element.14), channel_id=1, replica_groups=mesh['dp'=4,'vocab'=8] {'dp','vocab'}, use_global_device_ids=true, to_apply=%region_1.0 | all-reduce | flops 128 | bytes 1024 | tf_op jit(solution)/shard_map/pmax | solution.py:28
  138.4 2.1 exponential_reduce_fusion
  140.6 40.9 %all-reduce.2 = (f32[128]{0:T(128)S(1)}, f32[128]{0:T(128)S(1)}) all-reduce(f32[128]{0:T(128)S(1)} %get-tuple-element.4, f32[128]{0:T(128)S(1)} %exponential_multiply_fusion), channel_id=1, replica_groups=mesh['dp'=4,'vocab'=8] {'dp','vocab'}, use_global_device_ids=true, to_apply=%region_5.6 | all-reduce | flops 256 | bytes 2048 | tf_op jit(solution)/shard_map/psum | solution.py:41
  181.4 0.0 collective-permute-done
  181.4 0.0 copy-done
  181.4 0.0 copy-done.1
  181.4 1.2 fusion.1
  182.6 0.1 select_reduce_fusion.1
  182.7 39.1 %all-reduce.1 = (f32[8]{0:T(128)}, f32[8]{0:T(128)}) all-reduce(f32[8]{0:T(128)S(1)} %get-tuple-element.6, f32[8]{0:T(128)S(1)} %get-tuple-element.5), channel_id=1, replica_groups=mesh['dp'=4,'vocab'=8] {'dp','vocab'}, use_global_device_ids=true, to_apply=%region_8.9 | all-reduce | flops 16 | bytes 128 | tf_op jit(solution)/shard_map/psum | solution.py:58
  (3 shorter events, 0.0 us)
Async XLA Ops:
  7.2 62.9 %all-gather.3.cloned.1.call-start = ((), (), s32[]{:S(2)}) async-start(), calls=%async_computation | async-start | bytes 2162688 | tf_op jit(solution)/shard_map/all_gather | solution.py:39
  8.5 172.9 %collective-permute-start = (s32[1]{0:T(128)}, s32[1]{0:T(128)}, u32[]{:S(2)}, u32[]{:S(2)}) collective-permute-start(s32[1]{0:T(128)} %add.33), channel_id=1, source_target_pairs={{1,0},{2,1},{3,2},{4,3},{5,4},{6,5},{7,6},{8,7},{9,8},{10,9},{11,1... | collective-permute-start | bytes 20 | tf_op jit(solution)/shard_map/ppermute | solution.py:14
  100.1 81.4 %copy-start = (s32[4]{0:T(128)S(1)}, s32[4]{0:T(128)}, u32[]{:S(2)}) copy-start(s32[4]{0:T(128)} %param.10) | copy-start | bytes 52
  100.1 81.4 %copy-start.1 = (s32[4]{0:T(128)S(1)}, s32[4]{0:T(128)}, u32[]{:S(2)}) copy-start(s32[4]{0:T(128)} %param.9) | copy-start | bytes 52
Sparse Core Ops, SparseCore 0:
  10.9 59.1 all-gather.2
where the time goes:
time: 229 us
  blocking collectives  163 us (71%)
  matrix products  27.4 us (12%)
  between operations  14.7 us (6%)
  waiting for transfers between devices  14.1 us (6%)
  other arithmetic  5.02 us (2%)
  local copies, waits for them, and re-layouts  3.4 us (1%)
    unnamed x1, blocking collectives  44.3 us
    psum x1, blocking collectives, body(): lax.psum((stats[1] * jnp.exp(stats[0] - top_all), stats[2]), ('dp', 'voca...  40.9 us
    psum x1, blocking collectives, body(): lax.psum((jnp.sum(bench_hot * weighted[:, None], axis=0), jnp.sum(bench_h...  39.1 us
    pmax x1, blocking collectives, global_top(): return lax.pmax(stats[0], ('dp', 'vocab'))  38.3 us
    dot_general x1, matrix products, shard_stats(): logits = jnp.dot(piece, lm_head, preferred_element_type=jnp.float32)  27.4 us
    all_gather x1, waiting for transfers between devices, body(): lax.all_gather(hidden, ('dp', 'vocab'), axis=0, tiled=True)  13.5 us
  transfers between devices with their start and end apart: 2, of which 1 were waited for; matrix products, arithmetic and copies ran while one was open for 15% of the time, Pallas kernels for 0%

commit v1 on v0

v1 whole, which is shorter than its diff:
```python
from functools import partial

import jax
import jax.numpy as jnp
from jax import lax
from jax.experimental import pallas as pl
from jax.experimental.pallas import tpu as pltpu
from jax.sharding import PartitionSpec as P

NBENCH = 8
AXES = ("dp", "vocab")
LANES = 128
ROWS = 16
KTILE = 512


def swap(value, axis, bit):
    count = lax.axis_size(axis)
    return lax.ppermute(value, axis, [(i, i ^ bit) for i in range(count)])


def bits_from(low, count):
    out = []
    while low < count:
        out.append(low)
        low *= 2
    return out


def doubling(value, rounds):
    for axis, bit in rounds:
        value = jnp.concatenate([value, swap(value, axis, bit)], axis=0)
    return value


def gather_orders(n_dp, n_voc):
    far = [("vocab", b) for b in bits_from(2, n_voc)]
    side = [("dp", b) for b in bits_from(2, n_dp)]
    near = [("vocab", 1)]
    core = [("dp", 1)]
    return far + side + near + core, far + near + side + core


def gather_half(part, rounds, packed):
    rows, width = part.shape
    value = doubling(part.reshape(1, rows * width // LANES, LANES), rounds[:packed])
    value = value.reshape(1, rows * value.shape[0], width)
    return doubling(value, rounds[packed:])


def digit(value, place):
    return (lax.shift_right_logical(value, 8 * place) & 255).astype(jnp.bfloat16)


def logits_kernel(perm, positions, tok_dev, steps_a, me_ref, xa_ref, xb_ref, meta_ref, w_ref, out_ref, x_ref, acc_ref):
    step = pl.program_id(0)
    blocks = xa_ref.shape[0]
    tokens = x_ref.shape[0]

    @pl.when(step < steps_a)
    def _():
        for i in range(blocks):
            x_ref[i * ROWS : (i + 1) * ROWS, :] = xa_ref[i]

    @pl.when(step >= steps_a)
    def _():
        for i in range(blocks):
            x_ref[i * ROWS : (i + 1) * ROWS, :] = xb_ref[perm[i]]

    product = lax.dot_general(
        x_ref[...], w_ref[...], (((1,), (1,)), ((), ())), preferred_element_type=jnp.float32
    )

    @pl.when(step == 0)
    def _():
        acc_ref[...] = product

    @pl.when(step > 0)
    def _():
        acc_ref[...] += product

    @pl.when(step == pl.num_programs(0) - 1)
    def _():
        me = me_ref[0]
        logits = acc_ref[...]
        top = jnp.max(logits, axis=1, keepdims=True)
        total = jnp.sum(jnp.exp(logits - top), axis=1, keepdims=True)
        meta = meta_ref[...].reshape(tokens, LANES).astype(jnp.float32)
        target = meta[:, 0:1] + 256.0 * meta[:, 1:2] + 65536.0 * meta[:, 2:3]
        wanted = target.astype(jnp.int32) - me * logits.shape[1]
        columns = lax.broadcasted_iota(jnp.int32, logits.shape, 1)
        picked = jnp.sum(jnp.where(columns == wanted, logits, 0.0), axis=1, keepdims=True)
        seg = meta[:, 3:4] + 256.0 * meta[:, 4:5]
        pad = meta[:, 5:6]
        place = lax.broadcasted_iota(jnp.int32, (tokens, tokens), 0)
        block = lax.div(place, tok_dev)
        mask = jnp.zeros_like(place)
        for r, pos in enumerate(positions):
            mask = mask + (((block >> r) & 1) << pos)
        canon = (mask ^ me) * tok_dev + lax.rem(place, tok_dev)
        hit = canon == lax.broadcasted_iota(jnp.int32, (tokens, tokens), 1)
        out_ref[...] = jnp.zeros_like(out_ref)
        for row, column in enumerate((top, total, picked, seg, pad)):
            out_ref[row : row + 1, :] = jnp.sum(jnp.where(hit, column, 0.0), axis=0, keepdims=True)


def finish_kernel(all_ref, seq_ref, nll_ref, total_ref, count_ref):
    stats = all_ref[...]
    tokens = stats.shape[2]
    tops = stats[:, 0, :]
    top = jnp.max(tops, axis=0, keepdims=True)
    total = jnp.sum(stats[:, 1, :] * jnp.exp(tops - top), axis=0, keepdims=True)
    picked = jnp.sum(stats[:, 2, :], axis=0, keepdims=True)
    nll = top + jnp.log(total) - picked
    seg = all_ref[0, 3:4, :]
    pad = all_ref[0, 4:5, :]
    lane = lax.broadcasted_iota(jnp.int32, (1, tokens), 1)
    following = jnp.where(lane == tokens - 1, -1.0, pltpu.roll(seg, tokens - 1, 1))
    keep = pad * jnp.where(seg == following, 1.0, 0.0)
    count = seq_ref.shape[0]
    hot = lax.broadcasted_iota(jnp.int32, (count, tokens), 0) == seg.astype(jnp.int32)
    bench = jnp.sum(jnp.where(hot, seq_ref[...], 0), axis=0, keepdims=True)
    mine = lax.broadcasted_iota(jnp.int32, (NBENCH, tokens), 0) == bench
    nll_ref[...] = nll
    eye = lax.broadcasted_iota(jnp.int32, (NBENCH, NBENCH), 0) == lax.broadcasted_iota(jnp.int32, (NBENCH, NBENCH), 1)
    for ref, value in ((total_ref, keep * nll), (count_ref, keep)):
        column = jnp.sum(jnp.where(mine, value, 0.0), axis=1, keepdims=True)
        ref[...] = jnp.sum(jnp.where(eye, column, 0.0), axis=0, keepdims=True)


def body(hidden, lm_head, targets, segment, pad_mask, seq_bench):
    tok_dev, width = hidden.shape
    voc_dev = lm_head.shape[1]
    n_dp, n_voc = lax.axis_size("dp"), lax.axis_size("vocab")
    devices = n_dp * n_voc
    tokens = tok_dev * devices
    own_index = lax.axis_index(AXES).astype(jnp.int32)

    meta = jnp.stack(
        [digit(targets, 0), digit(targets, 1), digit(targets, 2), digit(segment, 0), digit(segment, 1), digit(pad_mask, 0)],
        axis=1,
    )
    meta = jnp.pad(meta, ((0, 0), (0, LANES - meta.shape[1])))
    half = width // 2
    order_a, order_b = gather_orders(n_dp, n_voc)
    packed = (ROWS // tok_dev).bit_length() - 1
    xa = gather_half(jnp.concatenate([hidden[:, :half], meta], axis=1), order_a, packed)
    xb = gather_half(hidden[:, half:], order_b, packed)

    blocks = xa.shape[0]
    late_a, late_b = order_a[packed:], order_b[packed:]
    spot = [late_b.index(entry) for entry in late_a]
    perm = [sum(((i >> r) & 1) << spot[r] for r in range(len(spot))) for i in range(blocks)]
    positions = [
        (bit.bit_length() - 1) + (n_voc.bit_length() - 1 if axis == "dp" else 0) for axis, bit in order_a
    ]
    steps_a = half // KTILE
    steps = width // KTILE
    stats = pl.pallas_call(
        partial(logits_kernel, perm, positions, tok_dev, steps_a),
        out_shape=jax.ShapeDtypeStruct((8, tokens), jnp.float32),
        grid_spec=pltpu.PrefetchScalarGridSpec(
            num_scalar_prefetch=1,
            grid=(steps,),
            in_specs=[
                pl.BlockSpec((blocks, ROWS, KTILE), lambda k, me: (0, 0, jnp.minimum(k, steps_a - 1))),
                pl.BlockSpec((blocks, ROWS, KTILE), lambda k, me: (0, 0, jnp.maximum(k - steps_a, 0))),
                pl.BlockSpec((blocks, ROWS, LANES), lambda k, me: (0, 0, half // LANES)),
                pl.BlockSpec((voc_dev, KTILE), lambda k, me: (0, k)),
            ],
            out_specs=pl.BlockSpec((8, tokens), lambda k, me: (0, 0)),
            scratch_shapes=[
                pltpu.VMEM((tokens, KTILE), jnp.bfloat16),
                pltpu.VMEM((tokens, voc_dev), jnp.float32),
            ],
        ),
        compiler_params=pltpu.CompilerParams(dimension_semantics=("arbitrary",), vmem_limit_bytes=24 * 1024 * 1024),
        cost_estimate=pl.CostEstimate(
            flops=2 * tokens * width * voc_dev, bytes_accessed=2 * width * voc_dev, transcendentals=tokens * voc_dev
        ),
        name="logits_stats",
    )(own_index.reshape(1), xa, xb, xa, lm_head.T)

    spread = jnp.broadcast_to(stats[None], (devices,) + stats.shape)
    gathered = lax.all_to_all(spread, AXES, split_axis=0, concat_axis=0, tiled=True)
    nll, bench_total, bench_count = pl.pallas_call(
        finish_kernel,
        out_shape=(
            jax.ShapeDtypeStruct((1, tokens), jnp.float32),
            jax.ShapeDtypeStruct((1, NBENCH), jnp.float32),
            jax.ShapeDtypeStruct((1, NBENCH), jnp.float32),
        ),
        name="finish",
    )(gathered, seq_bench.reshape(-1, 1))
    token_nll = lax.dynamic_slice_in_dim(nll.reshape(tokens), own_index * tok_dev, tok_dev, 0)
    return (token_nll, bench_total.reshape(NBENCH), bench_count.reshape(NBENCH))


def solution(mesh):
    in_specs = (
        P(AXES, None),
        P(None, AXES),
        P(AXES),
        P(AXES),
        P(AXES),
        P(),
    )
    out_specs = (P(AXES), P(), P())
    return jax.shard_map(body, mesh=mesh, in_specs=in_specs, out_specs=out_specs, check_vma=False)
```

time: 229 us -> 82.8 us (0.36)
  blocking collectives: 163 us -> 0 us
  Pallas kernels: 0 us -> 35.7 us
  matrix products: 27.4 us -> 0 us
  starting transfers between devices: 1.33 us -> 19.1 us
  between operations: 14.7 us -> 0.77 us
  waiting for transfers between devices: 14.1 us -> 20.2 us
  other arithmetic: 5.02 us -> 1.83 us
    psum x2 -> x0, blocking collectives: 79.9 us -> none  [the longest x1 40.9 us: body(): lax.psum((stats[1] * jnp.exp(stats[0] - top_all), stats[2]), ('dp', 'voca...]
    unnamed x1 -> x0, blocking collectives: 44.3 us -> none
    pmax x1 -> x0, blocking collectives: 38.3 us -> none  [global_top(): return lax.pmax(stats[0], ('dp', 'vocab'))]
    pallas_call x0 -> x2, Pallas kernels: none -> 35.7 us  [the longest x1 34.1 us: body(): pl.pallas_call(partial(logits_kernel, perm, positions, tok_dev, steps_a),...]
    dot_general x1 -> x0, matrix products: 27.4 us -> none  [shard_stats(): logits = jnp.dot(piece, lm_head, preferred_element_type=jnp.float32)]
    all_gather x1 -> x0, waiting for transfers between devices: 13.5 us -> none  [body(): lax.all_gather(hidden, ('dp', 'vocab'), axis=0, tiled=True)]
    ppermute x1 -> x10, starting transfers between devices: 1.29 us -> 14.6 us  [swap(): return lax.ppermute(value, axis, [(i, i ^ bit) for i in range(count)])]
    ppermute x1 -> x10, waiting for transfers between devices: 0.01 us -> 13.1 us  [swap(): return lax.ppermute(value, axis, [(i, i ^ bit) for i in range(count)])]
  transfers between devices with their start and end apart: 2 -> 11, of which waited for: 1 -> 8; matrix products, arithmetic and copies ran while one was open for 15% -> 3% of each run, Pallas kernels for 0% -> 0%
where the time goes in v1:
time: 82.8 us; the launch traced here: 82.1 us
  Pallas kernels  35.7 us (43%)
  waiting for transfers between devices  20.2 us (24%)
  starting transfers between devices  19.1 us (23%)
  local copies, waits for them, and re-layouts  4.52 us (5%)
  other arithmetic  1.83 us (2%)
    pallas_call x1, Pallas kernels, body(): pl.pallas_call(partial(logits_kernel, perm, positions, tok_dev, steps_a),...  34.1 us
    ppermute x10, starting transfers between devices, swap(): return lax.ppermute(value, axis, [(i, i ^ bit) for i in range(count)])  14.6 us
    ppermute x10, waiting for transfers between devices, swap(): return lax.ppermute(value, axis, [(i, i ^ bit) for i in range(count)])  13.1 us
    all_to_all x1, waiting for transfers between devices, body(): lax.all_to_all(spread, AXES, split_axis=0, concat_axis=0, tiled=True)  7.1 us
    all_to_all x1, starting transfers between devices, body(): lax.all_to_all(spread, AXES, split_axis=0, concat_axis=0, tiled=True)  4.47 us
  transfers between devices with their start and end apart: 11, of which 8 were waited for; matrix products, arithmetic and copies ran while one was open for 3% of the time, Pallas kernels for 0%

profile of v1, /device:TPU:0, one launch (start us, length us, event | category | flops | bytes accessed | tf_op | source)
XLA Modules:
  0.0 82.1 jit_solution(9199048103560808389)
XLA Ops:
  0.6 0.8 fusion.2
  1.5 3.1 %collective-permute-start.5 = (bf16[1,128,128]{2,1,0:T(8,128)(2,1)S(1)}, bf16[1,128,128]{2,1,0:T(8,128)(2,1)S(1)}, u32[]{:S(2)}, u32[]{:S(2)}) collective-permute-start(bf16[1,128,128]{2,1,0:T(8,128)(2,1)S(1)} %reshape.36), channel_id=1, source_target_pairs={{0,2},{1,3},{2,0},{3,1},{4,6},{5,7},{6,4},{7,5},{8,10},{9,11},{10,... | collective-permute-start | bytes 98312 | tf_op jit(solution)/shard_map/ppermute | solution.py:19
  4.6 0.7 convert_bitcast_fusion.3
  5.3 0.7 convert_bitcast_fusion.1
  6.0 0.1 copy.13
  6.1 0.1 collective-permute-start
  6.2 0.3 collective-permute-done.5
  6.5 3.1 %collective-permute-start.6 = (bf16[2,128,128]{2,1,0:T(8,128)(2,1)S(1)}, bf16[2,128,128]{2,1,0:T(8,128)(2,1)S(1)}, u32[]{:S(2)}, u32[]{:S(2)}) collective-permute-start(bf16[2,128,128]{2,1,0:T(8,128)(2,1)S(1)} %pad_maximum_fusion.9), channel_id=1, source_target_pairs={{0,4},{1,5},{2,6},{3,7},{4,0},{5,1},{6,2},{7,3},{8,12},{9,13},{10,... | collective-permute-start | bytes 196616 | tf_op jit(solution)/shard_map/ppermute | solution.py:19
  9.6 0.9 %collective-permute-done = bf16[1,132,128]{2,1,0:T(8,128)(2,1)S(1)} collective-permute-done((bf16[1,132,128]{2,1,0:T(8,128)(2,1)S(1)}, bf16[1,132,128]{2,1,0:T(8,128)(2,1)S(1)}, u32[]{:S(2)}, u32[]{:S(2)}) %collective-permute-start) | collective-permute-done | bytes 33824 | tf_op jit(solution)/shard_map/ppermute | solution.py:19
  10.5 2.3 %collective-permute-start.1 = (bf16[2,132,128]{2,1,0:T(8,128)(2,1)S(1)}, bf16[2,132,128]{2,1,0:T(8,128)(2,1)S(1)}, u32[]{:S(2)}, u32[]{:S(2)}) collective-permute-start(bf16[2,132,128]{2,1,0:T(8,128)(2,1)S(1)} %pad_maximum_fusion.8), channel_id=1, source_target_pairs={{0,4},{1,5},{2,6},{3,7},{4,0},{5,1},{6,2},{7,3},{8,12},{9,13},{10,... | collective-permute-start | bytes 202760 | tf_op jit(solution)/shard_map/ppermute | solution.py:19
  12.8 0.0 collective-permute-done.6
  12.8 0.1 reshape.37
  12.9 1.6 %collective-permute-start.7 = (bf16[1,16,4096]{2,1,0:T(8,128)(2,1)S(1)}, bf16[1,16,4096]{2,1,0:T(8,128)(2,1)S(1)}, u32[]{:S(2)}, u32[]{:S(2)}) collective-permute-start(bf16[1,16,4096]{2,1,0:T(8,128)(2,1)S(1)} %reshape.37), channel_id=1, source_target_pairs={{0,1},{1,0},{2,3},{3,2},{4,5},{5,4},{6,7},{7,6},{8,9},{9,8},{10,11... | collective-permute-start | bytes 393224 | tf_op jit(solution)/shard_map/ppermute | solution.py:19
  14.5 2.1 %collective-permute-done.1 = bf16[2,132,128]{2,1,0:T(8,128)(2,1)S(1)} collective-permute-done((bf16[2,132,128]{2,1,0:T(8,128)(2,1)S(1)}, bf16[2,132,128]{2,1,0:T(8,128)(2,1)S(1)}, u32[]{:S(2)}, u32[]{:S(2)}) %collective-permute-start.1) | collective-permute-done | bytes 67616 | tf_op jit(solution)/shard_map/ppermute | solution.py:19
  16.6 0.2 reshape.35
  16.8 1.6 %collective-permute-start.2 = (bf16[1,16,4224]{2,1,0:T(8,128)(2,1)S(1)}, bf16[1,16,4224]{2,1,0:T(8,128)(2,1)S(1)}, u32[]{:S(2)}, u32[]{:S(2)}) collective-permute-start(bf16[1,16,4224]{2,1,0:T(8,128)(2,1)S(1)} %reshape.35), channel_id=1, source_target_pairs={{0,16},{8,24},{16,0},{24,8},{1,17},{9,25},{17,1},{25,9},{2,18},{10... | collective-permute-start | bytes 405512 | tf_op jit(solution)/shard_map/ppermute | solution.py:19
  18.4 0.0 collective-permute-done.7
  18.4 1.1 %collective-permute-start.8 = (bf16[2,16,4096]{2,1,0:T(8,128)(2,1)S(1)}, bf16[2,16,4096]{2,1,0:T(8,128)(2,1)S(1)}, u32[]{:S(2)}, u32[]{:S(2)}) collective-permute-start(bf16[2,16,4096]{2,1,0:T(8,128)(2,1)S(1)} %pad_maximum_fusion.5), channel_id=1, source_target_pairs={{0,16},{8,24},{16,0},{24,8},{1,17},{9,25},{17,1},{25,9},{2,18},{10... | collective-permute-start | bytes 786440 | tf_op jit(solution)/shard_map/ppermute | solution.py:19
  19.5 3.2 %collective-permute-done.2 = bf16[1,16,4224]{2,1,0:T(8,128)(2,1)S(1)} collective-permute-done((bf16[1,16,4224]{2,1,0:T(8,128)(2,1)S(1)}, bf16[1,16,4224]{2,1,0:T(8,128)(2,1)S(1)}, u32[]{:S(2)}, u32[]{:S(2)}) %collective-permute-start.2) | collective-permute-done | bytes 135200 | tf_op jit(solution)/shard_map/ppermute | solution.py:19
  22.8 1.6 %collective-permute-start.3 = (bf16[2,16,4224]{2,1,0:T(8,128)(2,1)S(1)}, bf16[2,16,4224]{2,1,0:T(8,128)(2,1)S(1)}, u32[]{:S(2)}, u32[]{:S(2)}) collective-permute-start(bf16[2,16,4224]{2,1,0:T(8,128)(2,1)S(1)} %pad_maximum_fusion.4), channel_id=1, source_target_pairs={{0,1},{1,0},{2,3},{3,2},{4,5},{5,4},{6,7},{7,6},{8,9},{9,8},{10,11... | collective-permute-start | bytes 811016 | tf_op jit(solution)/shard_map/ppermute | solution.py:19
  24.4 1.2 %collective-permute-done.8 = bf16[2,16,4096]{2,1,0:T(8,128)(2,1)S(1)} collective-permute-done((bf16[2,16,4096]{2,1,0:T(8,128)(2,1)S(1)}, bf16[2,16,4096]{2,1,0:T(8,128)(2,1)S(1)}, u32[]{:S(2)}, u32[]{:S(2)}) %collective-permute-start.8) | collective-permute-done | bytes 262176 | tf_op jit(solution)/shard_map/ppermute | solution.py:19
  25.5 0.1 pad_maximum_fusion.3
  25.6 0.1 collective-permute-start.9
  25.7 3.6 %collective-permute-done.3 = bf16[2,16,4224]{2,1,0:T(8,128)(2,1)S(1)} collective-permute-done((bf16[2,16,4224]{2,1,0:T(8,128)(2,1)S(1)}, bf16[2,16,4224]{2,1,0:T(8,128)(2,1)S(1)}, u32[]{:S(2)}, u32[]{:S(2)}) %collective-permute-start.3) | collective-permute-done | bytes 270368 | tf_op jit(solution)/shard_map/ppermute | solution.py:19
  29.3 0.1 pad_maximum_fusion.2
  29.4 0.1 collective-permute-start.4
  29.5 0.0 collective-permute-done.9
  29.5 0.1 pad_maximum_fusion.1.xb_ref
  29.6 1.8 %collective-permute-done.4 = bf16[4,16,4224]{2,1,0:T(8,128)(2,1)S(1)} collective-permute-done((bf16[4,16,4224]{2,1,0:T(8,128)(2,1)S(1)}, bf16[4,16,4224]{2,1,0:T(8,128)(2,1)S(1)}, u32[]{:S(2)}, u32[]{:S(2)}) %collective-permute-start.4) | collective-permute-done | bytes 540704 | tf_op jit(solution)/shard_map/ppermute | solution.py:19
  31.4 0.1 pad_maximum_fusion.xa_ref.meta_ref
  31.5 0.0 copy-start.1
  31.5 34.1 %logits_stats.1 = f32[8,128]{1,0:T(8,128)S(1)} custom-call(s32[1]{0:T(128)} %bitcast.me_ref, bf16[8,16,4224]{2,1,0:T(8,128)(2,1)S(1)} %pad_maximum_fusion.xa_ref.meta_ref, bf16[8,16,4096]{2,1,0:T(8,128)(2,1)S(1)} %pad_maximum_fusion.1.xb_ref, bf16[8,16,4224]{2,1,0:T(8,128)(2,1)S(1)} %pad_maximum_fusion.xa_ref.meta_ref, bf16[4008,8192]{1,0:T(8,128)(2,1)} %bitcast.19), custom_call_target="tpu_custom_call" | custom-call | flops 8405385216 | bytes 65667072 | tf_op jit(solution)/shard_map/logits_stats/pallas_call | solution.py:159
  65.7 0.7 broadcast_in_dim.2
  66.3 4.5 %all-to-all-start = ((f32[32,8,128]{2,1,0:T(8,128)}), f32[32,8,128]{2,1,0:T(8,128)S(1)}, u32[]{:S(2)}, u32[]{:S(2)}) async-start(f32[32,8,128]{2,1,0:T(8,128)} %broadcast_in_dim.2), calls=%async_computation | async-start | bytes 262144 | tf_op jit(solution)/shard_map/all_to_all | solution.py:185
  70.8 0.0 copy-done.1
  70.8 0.7 copy.12.seq_ref
  71.5 7.1 %all-to-all-done.all_ref = f32[32,8,128]{2,1,0:T(8,128)S(1)} async-done(((f32[32,8,128]{2,1,0:T(8,128)}), f32[32,8,128]{2,1,0:T(8,128)S(1)}, u32[]{:S(2)}, u32[]{:S(2)}) %all-to-all-start) | async-done | bytes 131104 | tf_op jit(solution)/shard_map/all_to_all | solution.py:185
  78.6 0.0 copy-start
  78.6 0.7 copy-done
  79.3 1.6 %finish.1 = (f32[1,128]{1,0:T(1,128)}, f32[1,8]{1,0:T(1,128)}, f32[1,8]{1,0:T(1,128)}) custom-call(f32[32,8,128]{2,1,0:T(8,128)} %copy-done, s32[33,1]{1,0:T(8,128)} %copy.12.seq_ref), custom_call_target="tpu_custom_call" | custom-call | tf_op jit(solution)/shard_map/finish/pallas_call | solution.py:186
  80.9 1.2 %dynamic-slice_bitcast_fusion = f32[4]{0:T(128)} fusion(f32[1,128]{1,0:T(1,128)} %get-tuple-element.6, s32[]{:T(128)S(6)} %select_n.3), kind=kLoop, calls=%fused_computation.13 | loop fusion | bytes 36 | tf_op jit(solution)/shard_map/dynamic_slice | solution.py:195
  (10 shorter events, 0.2 us)
Async XLA Ops:
  1.5 5.0 %collective-permute-start.5 = (bf16[1,128,128]{2,1,0:T(8,128)(2,1)S(1)}, bf16[1,128,128]{2,1,0:T(8,128)(2,1)S(1)}, u32[]{:S(2)}, u32[]{:S(2)}) collective-permute-start(bf16[1,128,128]{2,1,0:T(8,128)(2,1)S(1)} %reshape.36), channel_id=1, source_target_pairs={{0,2},{1,3},{2,0},{3,1},{4,6},{5,7},{6,4},{7,5},{8,10},{9,11},{10,... | collective-permute-start | bytes 98312 | tf_op jit(solution)/shard_map/ppermute | solution.py:19
  6.1 4.4 %collective-permute-start = (bf16[1,132,128]{2,1,0:T(8,128)(2,1)S(1)}, bf16[1,132,128]{2,1,0:T(8,128)(2,1)S(1)}, u32[]{:S(2)}, u32[]{:S(2)}) collective-permute-start(bf16[1,132,128]{2,1,0:T(8,128)(2,1)S(1)} %reshape.34), channel_id=1, source_target_pairs={{0,2},{1,3},{2,0},{3,1},{4,6},{5,7},{6,4},{7,5},{8,10},{9,11},{10,... | collective-permute-start | bytes 101384 | tf_op jit(solution)/shard_map/ppermute | solution.py:19
  6.5 6.3 %collective-permute-start.6 = (bf16[2,128,128]{2,1,0:T(8,128)(2,1)S(1)}, bf16[2,128,128]{2,1,0:T(8,128)(2,1)S(1)}, u32[]{:S(2)}, u32[]{:S(2)}) collective-permute-start(bf16[2,128,128]{2,1,0:T(8,128)(2,1)S(1)} %pad_maximum_fusion.9), channel_id=1, source_target_pairs={{0,4},{1,5},{2,6},{3,7},{4,0},{5,1},{6,2},{7,3},{8,12},{9,13},{10,... | collective-permute-start | bytes 196616 | tf_op jit(solution)/shard_map/ppermute | solution.py:19
  10.5 6.0 %collective-permute-start.1 = (bf16[2,132,128]{2,1,0:T(8,128)(2,1)S(1)}, bf16[2,132,128]{2,1,0:T(8,128)(2,1)S(1)}, u32[]{:S(2)}, u32[]{:S(2)}) collective-permute-start(bf16[2,132,128]{2,1,0:T(8,128)(2,1)S(1)} %pad_maximum_fusion.8), channel_id=1, source_target_pairs={{0,4},{1,5},{2,6},{3,7},{4,0},{5,1},{6,2},{7,3},{8,12},{9,13},{10,... | collective-permute-start | bytes 202760 | tf_op jit(solution)/shard_map/ppermute | solution.py:19
  12.9 5.5 %collective-permute-start.7 = (bf16[1,16,4096]{2,1,0:T(8,128)(2,1)S(1)}, bf16[1,16,4096]{2,1,0:T(8,128)(2,1)S(1)}, u32[]{:S(2)}, u32[]{:S(2)}) collective-permute-start(bf16[1,16,4096]{2,1,0:T(8,128)(2,1)S(1)} %reshape.37), channel_id=1, source_target_pairs={{0,1},{1,0},{2,3},{3,2},{4,5},{5,4},{6,7},{7,6},{8,9},{9,8},{10,11... | collective-permute-start | bytes 393224 | tf_op jit(solution)/shard_map/ppermute | solution.py:19
  16.8 6.0 %collective-permute-start.2 = (bf16[1,16,4224]{2,1,0:T(8,128)(2,1)S(1)}, bf16[1,16,4224]{2,1,0:T(8,128)(2,1)S(1)}, u32[]{:S(2)}, u32[]{:S(2)}) collective-permute-start(bf16[1,16,4224]{2,1,0:T(8,128)(2,1)S(1)} %reshape.35), channel_id=1, source_target_pairs={{0,16},{8,24},{16,0},{24,8},{1,17},{9,25},{17,1},{25,9},{2,18},{10... | collective-permute-start | bytes 405512 | tf_op jit(solution)/shard_map/ppermute | solution.py:19
  18.4 7.1 %collective-permute-start.8 = (bf16[2,16,4096]{2,1,0:T(8,128)(2,1)S(1)}, bf16[2,16,4096]{2,1,0:T(8,128)(2,1)S(1)}, u32[]{:S(2)}, u32[]{:S(2)}) collective-permute-start(bf16[2,16,4096]{2,1,0:T(8,128)(2,1)S(1)} %pad_maximum_fusion.5), channel_id=1, source_target_pairs={{0,16},{8,24},{16,0},{24,8},{1,17},{9,25},{17,1},{25,9},{2,18},{10... | collective-permute-start | bytes 786440 | tf_op jit(solution)/shard_map/ppermute | solution.py:19
  22.8 6.5 %collective-permute-start.3 = (bf16[2,16,4224]{2,1,0:T(8,128)(2,1)S(1)}, bf16[2,16,4224]{2,1,0:T(8,128)(2,1)S(1)}, u32[]{:S(2)}, u32[]{:S(2)}) collective-permute-start(bf16[2,16,4224]{2,1,0:T(8,128)(2,1)S(1)} %pad_maximum_fusion.4), channel_id=1, source_target_pairs={{0,1},{1,0},{2,3},{3,2},{4,5},{5,4},{6,7},{7,6},{8,9},{9,8},{10,11... | collective-permute-start | bytes 811016 | tf_op jit(solution)/shard_map/ppermute | solution.py:19
  25.6 3.9 %collective-permute-start.9 = (bf16[4,16,4096]{2,1,0:T(8,128)(2,1)S(1)}, bf16[4,16,4096]{2,1,0:T(8,128)(2,1)S(1)}, u32[]{:S(2)}, u32[]{:S(2)}) collective-permute-start(bf16[4,16,4096]{2,1,0:T(8,128)(2,1)S(1)} %pad_maximum_fusion.3), channel_id=1, source_target_pairs={{0,8},{8,0},{16,24},{24,16},{1,9},{9,1},{17,25},{25,17},{2,10},{10... | collective-permute-start | bytes 1572872 | tf_op jit(solution)/shard_map/ppermute | solution.py:19
  29.4 2.0 %collective-permute-start.4 = (bf16[4,16,4224]{2,1,0:T(8,128)(2,1)S(1)}, bf16[4,16,4224]{2,1,0:T(8,128)(2,1)S(1)}, u32[]{:S(2)}, u32[]{:S(2)}) collective-permute-start(bf16[4,16,4224]{2,1,0:T(8,128)(2,1)S(1)} %pad_maximum_fusion.2), channel_id=1, source_target_pairs={{0,8},{8,0},{16,24},{24,16},{1,9},{9,1},{17,25},{25,17},{2,10},{10... | collective-permute-start | bytes 1622024 | tf_op jit(solution)/shard_map/ppermute | solution.py:19
  31.5 39.3 %copy-start.1 = (s32[33]{0:T(128)S(1)}, s32[33]{0:T(128)}, u32[]{:S(2)}) copy-start(s32[33]{0:T(128)} %param.11) | copy-start | bytes 400
  66.3 12.3 %all-to-all-start = ((f32[32,8,128]{2,1,0:T(8,128)}), f32[32,8,128]{2,1,0:T(8,128)S(1)}, u32[]{:S(2)}, u32[]{:S(2)}) async-start(f32[32,8,128]{2,1,0:T(8,128)} %broadcast_in_dim.2), calls=%async_computation | async-start | bytes 262144 | tf_op jit(solution)/shard_map/all_to_all | solution.py:185
  78.6 0.7 copy-start
